TPU v7x, 32 devices: a whole 2x2x4 slice. The times are simulated.
32 devices in a mesh: tp: 4 (over z), dp: 8 (over y, x, core).
Axes of the slice: x: 2, y: 2, z: 4, core: 2. Of those that a mesh axis runs over, the one named last changes fastest.
Arguments:
- hidden: bfloat16 [32, 512, 5120], P('dp')
- gain_in: float32 [5120], replicated
- gain_q: float32 [1536], replicated
- gain_kv: float32 [512], replicated
- w_qa: bfloat16 [5120, 1536], replicated
- w_kva: bfloat16 [5120, 576], replicated
- w_qb: bfloat16 [1536, 24576], P(None, 'tp')
- w_kvb: bfloat16 [512, 32768], P(None, 'tp')
- w_out: bfloat16 [16384, 5120], P('tp')
Outputs:
- output 1: bfloat16 [32, 512, 5120], P('dp')
- output 2: float32 [128], replicated
- output 3: bfloat16 [1536, 24576], P(None, 'tp')
- output 4: bfloat16 [512, 32768], P(None, 'tp')
All inputs are finite; a program needn't handle non-finite values.
Results may differ from a plain program's by a relative error of at most 0.00727548.
Values sent between devices are 32-bit elements.
A program may use at most 1 GiB of HBM per device.

v0:
```python
import math
import jax
import jax.numpy as jnp
from jax import lax
from jax.sharding import PartitionSpec as P

NORM_EPS = 1e-6
ROPE_BASE = 50000.0
MSCALE_SQ = (0.1 * math.log(32.0) + 1.0) ** 2
CLIP_TAU = 100.0


def rms_norm(tensor, gain_vec):
    return tensor * lax.rsqrt(jnp.mean(tensor * tensor, axis=-1, keepdims=True) + NORM_EPS) * gain_vec


def rope_tables(positions, rope_dim):
    inv_freq = ROPE_BASE ** (-2.0 * jnp.arange(rope_dim // 2, dtype=jnp.float32) / rope_dim)
    angles = positions.astype(jnp.float32)[:, None] * inv_freq[None, :]
    return jnp.cos(angles), jnp.sin(angles)


def rotate(tensor, cos_table, sin_table):
    half_dim = tensor.shape[-1] // 2
    first_half = tensor[..., :half_dim]
    second_half = tensor[..., half_dim:]
    return jnp.concatenate([first_half * cos_table - second_half * sin_table, first_half * sin_table + second_half * cos_table], axis=-1)


def head_dims(kv_rank, kva_cols, qb_cols, kvb_cols, out_rows):
    rope_dim = kva_cols - kv_rank
    num_heads = (qb_cols - kvb_cols + out_rows) // rope_dim
    return rope_dim, num_heads, (kvb_cols - out_rows) // num_heads, out_rows // num_heads


def column_gains(first_gain, first_dim, second_gain, second_dim):
    num_heads = first_gain.shape[0]
    return jnp.concatenate([jnp.broadcast_to(first_gain[:, None], (num_heads, first_dim)), jnp.broadcast_to(second_gain[:, None], (num_heads, second_dim))], axis=1).reshape(-1)


def rescale(weight, col_gain):
    return (weight.astype(jnp.float32) * col_gain[None, :]).astype(jnp.bfloat16)


def solution(mesh):
    def device_step(hidden, gain_in, gain_q, gain_kv, w_qa, w_kva, w_qb, w_kvb, w_out):
        num_seqs, seq_len, model_dim = hidden.shape
        kv_rank = gain_kv.shape[0]
        rope_dim, num_heads, nope_dim, value_dim = head_dims(kv_rank, w_kva.shape[1], w_qb.shape[1], w_kvb.shape[1], w_out.shape[0])
        logit_scale = (nope_dim + rope_dim) ** -0.5 * MSCALE_SQ
        positions = jnp.arange(seq_len)
        cos_table, sin_table = rope_tables(positions, rope_dim)
        causal = positions[:, None] >= positions[None, :]
        normed = rms_norm(hidden.astype(jnp.float32), gain_in).astype(jnp.bfloat16)
        q_lat = rms_norm(jnp.einsum('bsd,dr->bsr', normed, w_qa, preferred_element_type=jnp.float32), gain_q).astype(jnp.bfloat16)
        kv_lat = jnp.einsum('bsd,dr->bsr', normed, w_kva, preferred_element_type=jnp.float32)
        latent = rms_norm(kv_lat[..., :kv_rank], gain_kv).astype(jnp.bfloat16)
        k_rot = rotate(kv_lat[..., kv_rank:], cos_table, sin_table).astype(jnp.bfloat16)
        q_full = jnp.einsum('bsr,rc->bsc', q_lat, w_qb, preferred_element_type=jnp.float32).reshape(num_seqs, seq_len, num_heads, nope_dim + rope_dim)
        q_nope = q_full[..., :nope_dim].astype(jnp.bfloat16)
        q_rot = rotate(q_full[..., nope_dim:], cos_table[:, None, :], sin_table[:, None, :]).astype(jnp.bfloat16)
        kv_full = jnp.einsum('bsr,rc->bsc', latent, w_kvb, preferred_element_type=jnp.float32).astype(jnp.bfloat16).reshape(num_seqs, seq_len, num_heads, nope_dim + value_dim)
        logits = jnp.einsum('bqhd,bkhd->bhqk', q_nope, kv_full[..., :nope_dim], preferred_element_type=jnp.float32) + jnp.einsum('crie,cle->cirl', q_rot, k_rot, preferred_element_type=jnp.float32)
        logits = jnp.where(causal, logits * logit_scale, -jnp.inf)
        local_max = jnp.max(logits, axis=(0, 2, 3))
        attn_prob = jax.nn.softmax(logits, axis=-1).astype(jnp.bfloat16)
        attn_out = jnp.einsum('bhqk,bkhd->bqhd', attn_prob, kv_full[..., nope_dim:], preferred_element_type=jnp.float32).astype(jnp.bfloat16)
        head_part = jnp.einsum('crd,de->cre', attn_out.reshape(num_seqs, seq_len, num_heads * value_dim), w_out, preferred_element_type=jnp.float32)
        head_sum = lax.psum(head_part, 'tp')
        out_hidden = (hidden.astype(jnp.float32) + head_sum).astype(jnp.bfloat16)
        head_max = lax.pmax(local_max, 'dp')
        clip_gain = CLIP_TAU / jnp.maximum(CLIP_TAU, head_max)
        root_gain = jnp.sqrt(clip_gain)
        new_qb = rescale(w_qb, column_gains(root_gain, nope_dim, clip_gain, rope_dim))
        new_kvb = rescale(w_kvb, column_gains(root_gain, nope_dim, jnp.ones_like(clip_gain), value_dim))
        logit_max = lax.all_gather(head_max, 'tp', tiled=True)
        return out_hidden, logit_max, new_qb, new_kvb

    weight_spec = P(None, 'tp')
    return jax.shard_map(device_step, mesh=mesh, in_specs=(P('dp', None, None), P(), P(), P(), P(), P(), weight_spec, weight_spec, P('tp', None)), out_specs=(P('dp', None, None), P(), weight_spec, weight_spec), check_vma=False)
```

profile of v0, /device:TPU:0, one launch (start us, length us, event | category | flops | bytes accessed | tf_op | source)
XLA Modules:
  0.0 2054.4 jit_solution(10998436859814718921)
XLA Ops:
  7.2 0.0 all-reduce.4.cloned.1.call-start
  7.2 0.8 iota_compare_fusion
  8.0 8.8 fusion.4
  16.9 42.3 %multiply_reduce_fusion = (f32[4,512]{1,0:T(4,128)S(1)}, f32[4,512,1536]{2,1,0:T(8,128)}) fusion(bf16[5120,1536]{1,0:T(8,128)(2,1)} %param.13, bf16[4,512,5120]{2,1,0:T(8,128)(2,1)} %param.9, f32[5120]{0:T(1024)S(1)} %copy-done.3, f32[4,512]{1,0:T(4,128)S(1)} %add_rsqrt_fusion.2), kind=kOutput, calls=%fused_computation.28 | convolution fusion | flops 32260487168 | bytes 49319936 | tf_op jit(solution)/shard_map/bsd,dr->bsr/dot_general | solution.py:55
  59.3 17.6 fusion.16
  76.9 0.5 multiply_reduce_fusion.1
  77.5 0.3 multiply_cosine_fusion
  77.8 1.3 copy-done.1
  79.1 0.1 subtract_convert_fusion.1
  79.2 51.3 %fusion.10 = f32[4,512,6144]{1,2,0:T(8,128)} fusion(bf16[1536,6144]{1,0:T(8,128)(2,1)} %param.15, f32[4,512,1536]{2,1,0:T(8,128)} %get-tuple-element.15, f32[1536]{0:T(1024)S(1)} %copy-done.4, f32[4,512]{1,0:T(4,128)S(1)} %add_rsqrt_fusion), kind=kOutput, calls=%fused_computation.19 | convolution fusion | flops 38664142848 | bytes 81803264 | tf_op jit(solution)/shard_map/bsr,rc->bsc/dot_general | solution.py:59
  130.5 9.6 subtract_convert_fusion
  140.2 1.7 slice-done.1
  141.9 24.5 %convolution_convert_fusion = bf16[4,512,8192]{2,1,0:T(8,128)(2,1)} fusion(bf16[512,8192]{1,0:T(8,128)(2,1)S(1)} %bitcast.50, f32[4,512,576]{1,2,0:T(8,128)} %copy-done.1, f32[512]{0:T(512)S(1)} %copy-done.5, f32[4,512]{1,0:T(4,128)S(1)} %add_rsqrt_fusion.1), kind=kOutput, calls=%fused_computation.18 | convolution fusion | flops 17199792128 | bytes 46147584 | tf_op jit(solution)/shard_map/bsr,rc->bsc/dot_general | solution.py:62
  166.4 23.0 %copy.43 = bf16[256,8,32,256]{3,2,1,0:T(8,128)(2,1)} copy(bf16[256,8,32,256]{3,1,2,0:T(8,128)(2,1)} %bitcast.48) | data formatting | bytes 67108864
  189.4 24.2 %fusion.36 = (bf16[4,512,32,128]{3,2,1,0:T(8,128)(2,1)}, bf16[4,512,32,128]{3,2,1,0:T(8,128)(2,1)}) fusion(bf16[4,512,32,256]{3,2,1,0:T(8,128)(2,1)} %bitcast.45), kind=kLoop, calls=%fused_computation.62 | loop fusion | bytes 67108864 | tf_op jit(solution)/shard_map/slice | solution.py:67
  213.6 47.1 %fusion.22 = f32[4,512,512,32]{2,1,3,0:T(8,128)} fusion(bf16[4,512,32,32]{1,3,2,0:T(8,128)(2,1)} %get-tuple-element.7, bf16[4,512,32,32]{1,3,2,0:T(8,128)(2,1)} %get-tuple-element.6, bf16[4,512,32]{1,2,0:T(8,128)(2,1)S(1)} %get-tuple-element.11, bf16[4,512,32]{1,2,0:T(8,128)(2,1)S(1)} %get-tuple-element.10), kind=kOutput, calls=%fused_computation.30 | convolution fusion | flops 4312268800 | bytes 142868480 | tf_op jit(solution)/shard_map/crie,cle->cirl/dot_general | solution.py:63
  260.7 103.1 %fusion.38 = (f32[32]{0:T(128)}, f32[4,32,512,512]{2,3,1,0:T(8,128)}) fusion(f32[4,512,512,32]{2,1,3,0:T(8,128)} %fusion.22, f32[4,512,32,192]{1,3,2,0:T(8,128)} %bitcast.47, bf16[4,512,32,128]{3,2,1,0:T(8,128)(2,1)} %get-tuple-element.9, pred[512,512]{0,1:T(8,128)(4,1)S(1)} %copy-done), kind=kOutput, calls=%fused_computation.64 | convolution fusion | flops 8724152320 | bytes 302252160 | tf_op jit(solution)/shard_map/bqhd,bkhd->bhqk/dot_general | solution.py:63
  363.7 128.5 %fusion.37 = (f32[4,32,512]{2,1,0:T(8,128)S(1)}, f32[4,32,512,512]{2,3,1,0:T(8,128)}) fusion(f32[4,32,512,512]{2,3,1,0:T(8,128)} %get-tuple-element.19), kind=kOutput, calls=%fused_computation.63 | output fusion | flops 67109376 | bytes 268697600 | tf_op jit(solution)/shard_map/sub | solution.py:66
  492.3 53.1 %fusion.19 = bf16[4,32,128,512]{3,2,1,0:T(8,128)(2,1)} fusion(f32[4,32,512,512]{2,3,1,0:T(8,128)} %get-tuple-element.17, f32[4,32,512]{2,1,0:T(8,128)S(1)} %get-tuple-element.16, bf16[4,512,32,128]{3,2,1,0:T(8,128)(2,1)} %get-tuple-element.8), kind=kOutput, calls=%fused_computation.29 | convolution fusion | flops 8665432064 | bytes 168034304 | tf_op jit(solution)/shard_map/bhqk,bkhd->bqhd/dot_general | solution.py:67
  545.4 99.6 %fusion.8 = f32[4,512,5120]{2,1,0:T(8,128)} fusion(bf16[4,512,4096]{1,2,0:T(8,128)(2,1)} %bitcast.52, bf16[4096,5120]{1,0:T(8,128)(2,1)} %param.17), kind=kOutput, calls=%fused_computation.14 | convolution fusion | flops 85899345920 | bytes 100663296 | tf_op jit(solution)/shard_map/crd,de->cre/dot_general | solution.py:68
  645.0 0.6 copy-done.2
  645.6 15.6 pmax.7
  661.2 0.1 broadcast_in_dim.13
  661.3 0.1 broadcast_in_dim.12
  661.4 0.1 mul.251
  661.5 0.6 dynamic-slice
  662.8 0.2 dynamic-update-slice
  663.0 15.0 all-reduce.1
  678.0 8.9 multiply_convert_fusion.1
  686.9 18.2 multiply_convert_fusion
  705.1 1314.5 %all-reduce.4.cloned.1.call-done = f32[4,512,5120]{2,1,0:T(8,128)} async-done(((f32[4,512,5120]{2,1,0:T(8,128)}), f32[4,512,5120]{2,1,0:T(8,128)}) %all-reduce.4.cloned.1.call-update) | async-done | bytes 41943056 | tf_op jit(solution)/shard_map/psum | solution.py:69
  2019.6 27.5 %fusion.7 = bf16[4,512,5120]{2,1,0:T(8,128)(2,1)} fusion(f32[4,512,5120]{2,1,0:T(8,128)} %all-reduce.4.cloned.1.call-done, bf16[4,512,5120]{2,1,0:T(8,128)(2,1)} %param.9), kind=kLoop, calls=%fused_computation.13 | loop fusion | flops 31457280 | bytes 83886080 | tf_op jit(solution)/shard_map/convert_element_type | solution.py:70
  (27 shorter events, 0.1 us)
Async XLA Ops:
  7.2 9.7 copy-start.3
  7.2 2012.4 %all-reduce.4.cloned.1.call-start = ((), (), s32[]{:S(2)}) async-start(), calls=%async_computation | async-start | bytes 83886080 | tf_op jit(solution)/shard_map/psum | solution.py:69
  59.3 19.9 copy-start.4
  76.9 2.2 copy-start.1
  130.5 9.7 slice-start
  130.5 9.7 copy-start.5
  130.5 11.4 slice-start.1
  213.6 47.1 %copy-start = (pred[512,512]{0,1:T(8,128)(4,1)S(1)}, pred[512,512]{0,1:T(8,128)(4,1)}, u32[]{:S(2)}) copy-start(pred[512,512]{0,1:T(8,128)(4,1)} %iota_compare_fusion) | copy-start | bytes 786436
  645.0 0.7 copy-start.2
  645.0 16.5 copy-start.6
Sparse Core Ops, SparseCore 0:
  645.1 1374.4 all-reduce.3
where the time goes:
time: 2060 us; the launch traced here: 2050 us
  waiting for transfers between devices  1310 us (64%)
  matrix products  439 us (21%)
  other arithmetic  203 us (10%)
  local copies, waits for them, and re-layouts  52 us (3%)
  blocking collectives  30.6 us (1%)
    psum x1, waiting for transfers between devices, device_step(): head_sum = lax.psum(head_part, 'tp')  1310 us
    sub x1, other arithmetic, device_step(): attn_prob = jax.nn.softmax(logits, axis=-1).astype(jnp.bfloat16)  129 us
    dot_general x1, matrix products, device_step(): jnp.einsum('bqhd,bkhd->bhqk', q_nope, kv_full[..., :nope_dim], preferred_...  103 us
    dot_general x1, matrix products, device_step(): jnp.einsum('crd,de->cre', attn_out.reshape(num_seqs, seq_len, num_heads *...  99.6 us
    dot_general x1, matrix products, device_step(): jnp.einsum('bhqk,bkhd->bqhd', attn_prob, kv_full[..., nope_dim:], preferr...  53.1 us
    dot_general x1, matrix products, device_step(): jnp.einsum('bsr,rc->bsc', q_lat, w_qb, preferred_element_type=jnp.float32)  51.3 us
    dot_general x1, matrix products, device_step(): jnp.einsum('crie,cle->cirl', q_rot, k_rot, preferred_element_type=jnp.flo...  47.1 us
    dot_general x1, matrix products, device_step(): jnp.einsum('bsd,dr->bsr', normed, w_qa, preferred_element_type=jnp.float32)  42.3 us
  transfers between devices with their start and end apart: 1, of which 1 were waited for; matrix products, arithmetic and copies ran while one was open for 1% of the time, Pallas kernels for 0%

commit v1 on v0

v1 whole, which is shorter than its diff:
```python
import math
import jax
import jax.numpy as jnp
from jax import lax
from jax.experimental import pallas as pl
from jax.experimental.pallas import tpu as pltpu
from jax.sharding import PartitionSpec as P

NORM_EPS = 1e-6
ROPE_BASE = 50000.0
MSCALE_SQ = (0.1 * math.log(32.0) + 1.0) ** 2
CLIP_TAU = 100.0
MESH = pl.DeviceIdType.MESH
F32 = jnp.float32
BF16 = jnp.bfloat16

TILE = 256
DEPTH = 512
LAG_PAIR, LAG_MID, LAG_END = 2, 4, 6
SLOTS_P, SLOTS_1, SLOTS_2, SLOTS_3, SLOTS_T = 5, 7, 6, 7, 3


def rope_tables(seq_len, rope_dim):
    inv_freq = ROPE_BASE ** (-2.0 * jnp.arange(rope_dim // 2, dtype=F32) / rope_dim)
    angles = jnp.arange(seq_len).astype(F32)[:, None] * inv_freq[None, :]
    cos, sin = jnp.cos(angles), jnp.sin(angles)
    blank = jnp.zeros((seq_len, 128 - rope_dim), F32)
    return jnp.concatenate([cos, cos, blank], axis=1), jnp.concatenate([-sin, sin, blank], axis=1)


def column_gains(first_gain, first_dim, second_gain, second_dim):
    num_heads = first_gain.shape[0]
    return jnp.concatenate([jnp.broadcast_to(first_gain[:, None], (num_heads, first_dim)), jnp.broadcast_to(second_gain[:, None], (num_heads, second_dim))], axis=1).reshape(-1)


def rescale(weight, col_gain):
    return (weight.astype(F32) * col_gain[None, :]).astype(BF16)


def dot(a, b):
    return jnp.dot(a, b, preferred_element_type=F32)


def kernel(dims, x_hbm, gin, gq, gkv, cos, sin, wqa_hbm, wkva_hbm, wqb_hbm, wkvb_hbm, wout_hbm,
           y_hbm, gall, gmine,
           xn, accq, acck, cq, ckv, krot, obuf, wqa, wkva, wqb, wkvb, wout,
           pbuf, r1, r2, r3, tbuf, xt, yt, smax, srecv,
           x_sem, a_sem, b_sem, o_sem, xt_sem, yt_sem,
           p_send, r1_recv, a_send, r2_recv, t_send, r3_recv, st_send, st_recv, g_send, g_recv):
    num_seqs, seq_len, model_dim, scale, rope_dim = dims
    q_rank = cq.shape[1]
    kv_rank = ckv.shape[1]
    tiles = model_dim // TILE
    units = model_dim // DEPTH
    pairs = wqb_hbm.shape[1] // 384
    total = num_seqs * tiles
    z = lax.axis_index("tp")
    dp = lax.axis_index("dp")
    is_mid = jnp.logical_or(z == 1, z == 2)
    is_end = jnp.logical_or(z == 0, z == 3)
    near = z + 1 - 2 * (z % 2)
    across = 3 - z
    dp_peer = [dp + 1 - 2 * (dp % 2), dp + 2 - 4 * ((dp // 2) % 2), dp + 4 - 8 * (dp // 4)]
    tp_peer = [(z + d) % 4 for d in (1, 2, 3)]

    barrier = pltpu.get_barrier_semaphore()
    for peer in dp_peer:
        pl.semaphore_signal(barrier, inc=1, device_id={"dp": peer}, device_id_type=MESH)
    for peer in tp_peer:
        pl.semaphore_signal(barrier, inc=1, device_id={"tp": peer}, device_id_type=MESH)
    pl.semaphore_wait(barrier, 6)

    def x_copy(seq):
        return pltpu.make_async_copy(x_hbm.at[seq], xn, x_sem)

    def a_copies(u):
        slot = u % 2
        rows = pl.ds(pl.multiple_of(u * DEPTH, DEPTH), DEPTH)
        return (pltpu.make_async_copy(wqa_hbm.at[rows], wqa.at[slot], a_sem.at[0, slot]),
                pltpu.make_async_copy(wkva_hbm.at[rows], wkva.at[slot], a_sem.at[1, slot]))

    def b_copies(hp):
        slot = hp % 2
        return (pltpu.make_async_copy(wqb_hbm.at[:, pl.ds(pl.multiple_of(hp * 384, 384), 384)], wqb.at[slot], b_sem.at[0, slot]),
                pltpu.make_async_copy(wkvb_hbm.at[:, pl.ds(pl.multiple_of(hp * 512, 512), 512)], wkvb.at[slot], b_sem.at[1, slot]))

    def cols_of(k):
        return pl.ds(pl.multiple_of((k % tiles) * TILE, TILE), TILE)

    def o_copy(k):
        return pltpu.make_async_copy(wout_hbm.at[:, cols_of(k)], wout.at[k % 2], o_sem.at[k % 2])

    def xt_copy(k):
        return pltpu.make_async_copy(x_hbm.at[k // tiles, :, cols_of(k)], xt, xt_sem)

    def yt_copy(k):
        return pltpu.make_async_copy(yt.at[k % 2], y_hbm.at[k // tiles, :, cols_of(k)], yt_sem.at[k % 2])

    def p_copy(k):
        return pltpu.make_async_remote_copy(
            src_ref=pbuf.at[k % SLOTS_P], dst_ref=r1.at[k % SLOTS_1], send_sem=p_send.at[k % SLOTS_P],
            recv_sem=r1_recv.at[k % SLOTS_1], device_id={"tp": near}, device_id_type=MESH)

    def a_copy(k):
        return pltpu.make_async_remote_copy(
            src_ref=pbuf.at[k % SLOTS_P], dst_ref=r2.at[k % SLOTS_2], send_sem=a_send.at[k % SLOTS_P],
            recv_sem=r2_recv.at[k % SLOTS_2], device_id={"tp": across}, device_id_type=MESH)

    def t_copy(k):
        return pltpu.make_async_remote_copy(
            src_ref=tbuf.at[k % SLOTS_T], dst_ref=r3.at[k % SLOTS_3], send_sem=t_send.at[k % SLOTS_T],
            recv_sem=r3_recv.at[k % SLOTS_3], device_id={"tp": near}, device_id_type=MESH)

    def st_copy(r):
        return pltpu.make_async_remote_copy(
            src_ref=smax, dst_ref=srecv.at[r], send_sem=st_send.at[r],
            recv_sem=st_recv.at[r], device_id={"dp": dp_peer[r]}, device_id_type=MESH)

    def g_copy(d):
        return pltpu.make_async_remote_copy(
            src_ref=smax, dst_ref=gall.at[z], send_sem=g_send.at[d],
            recv_sem=g_recv.at[d], device_id={"tp": tp_peer[d]}, device_id_type=MESH)

    def normalize():
        def block(i, carry):
            rows = pl.ds(pl.multiple_of(i * 16, 16), 16)
            v = xn[rows, :].astype(F32)
            inv = lax.rsqrt(jnp.mean(v * v, axis=-1, keepdims=True) + NORM_EPS)
            xn[rows, :] = (v * inv * gin[...]).astype(BF16)
            return carry
        lax.fori_loop(0, seq_len // 16, block, 0)

    def a_step(u):
        for c in a_copies(u):
            c.wait()

        @pl.when(u + 1 < units)
        def _():
            for c in a_copies(u + 1):
                c.start()

        slot = u % 2
        cols = pl.ds(pl.multiple_of(u * DEPTH, DEPTH), DEPTH)
        piece = xn[:, cols]
        width = 512

        @pl.when(u == 0)
        def _():
            for j in range(q_rank // width):
                accq[:, j * width:(j + 1) * width] = dot(piece, wqa[slot, :, j * width:(j + 1) * width])
            acck[...] = dot(piece, wkva[slot])

        @pl.when(u > 0)
        def _():
            for j in range(q_rank // width):
                accq[:, j * width:(j + 1) * width] += dot(piece, wqa[slot, :, j * width:(j + 1) * width])
            acck[...] += dot(piece, wkva[slot])

    def rope(v, c, s):
        half = rope_dim // 2
        lane = lax.broadcasted_iota(jnp.int32, v.shape, 1)
        swap = jnp.where(lane < half, pltpu.roll(v, 128 - half, 1), pltpu.roll(v, half, 1))
        return v * c + swap * s

    def finish_latents():
        def block(i, carry):
            rows = pl.ds(pl.multiple_of(i * 64, 64), 64)
            v = accq[rows, :]
            inv = lax.rsqrt(jnp.mean(v * v, axis=-1, keepdims=True) + NORM_EPS)
            cq[rows, :] = (v * inv * gq[...]).astype(BF16)
            w = acck[rows, :kv_rank]
            inv = lax.rsqrt(jnp.mean(w * w, axis=-1, keepdims=True) + NORM_EPS)
            ckv[rows, :] = (w * inv * gkv[...]).astype(BF16)
            kr = jnp.concatenate([acck[rows, kv_rank:], jnp.zeros((64, 128 - rope_dim), F32)], axis=1)
            krot[rows, :] = rope(kr, cos[rows, :], sin[rows, :]).astype(BF16)
            return carry
        lax.fori_loop(0, seq_len // 64, block, 0)

    def b_step(hp, oslot):
        for c in b_copies(hp):
            c.wait()

        @pl.when(hp + 1 < pairs)
        def _():
            for c in b_copies(hp + 1):
                c.start()

        slot = hp % 2
        qf = dot(cq[...], wqb[slot])
        kv = dot(ckv[...], wkvb[slot]).astype(BF16)
        qs = pltpu.roll(qf, 192, 1)
        blk = 256
        for head, q2 in ((0, qf), (1, qs)):
            q_rot = rope(q2[:, 128:256], cos[...], sin[...])
            qcat = jnp.concatenate([q2[:, :128].astype(BF16), q_rot.astype(BF16)], axis=1)
            kcat = jnp.concatenate([kv[:, head * 256:head * 256 + 128], krot[...]], axis=1)
            vals = kv[:, head * 256 + 128:head * 256 + 256]
            best = None
            for i in range(seq_len // blk):
                width = (i + 1) * blk
                l = lax.dot_general(qcat[i * blk:width], kcat[:width], (((1,), (1,)), ((), ())), preferred_element_type=F32) * scale
                row = lax.broadcasted_iota(jnp.int32, l.shape, 0) + i * blk
                col = lax.broadcasted_iota(jnp.int32, l.shape, 1)
                l = jnp.where(col <= row, l, -jnp.inf)
                m = jnp.max(l, axis=-1, keepdims=True)
                e = jnp.exp(l - m)
                p = (e * (1.0 / jnp.sum(e, axis=-1, keepdims=True))).astype(BF16)
                o = dot(p, vals[:width]).astype(BF16)
                obuf[oslot, i * blk:width, pl.ds(pl.multiple_of(hp * 256 + head * 128, 128), 128)] = o
                top = jnp.max(m, axis=0, keepdims=True)
                best = top if best is None else jnp.maximum(best, top)
            r = pl.ds(hp * 2 + head, 1)
            smax[r, :] = jnp.maximum(smax[r, :], jnp.broadcast_to(best, (1, 128)))

    def finish_tile(k, value):
        xt_copy(k).wait()

        @pl.when(k >= 2)
        def _():
            yt_copy(k - 2).wait()

        yt[k % 2] = (xt[...].astype(F32) + value).astype(BF16)
        yt_copy(k).start()

    smax[...] = jnp.full(smax.shape, -jnp.inf, F32)

    def tick(i):
        seq = i // tiles
        t = i % tiles
        tau = i - tiles

        done_tile = jnp.where(is_mid, tau - LAG_MID, tau - LAG_END)

        @pl.when(jnp.logical_and(done_tile >= 0, done_tile < total))
        def _():
            xt_copy(done_tile).start()

        @pl.when(i == 0)
        def _():
            o_copy(0).start()

        @pl.when(jnp.logical_and(is_end, jnp.logical_and(tau >= SLOTS_P, tau < total + SLOTS_P)))
        def _():
            p_copy(tau - SLOTS_P).wait_send()

        @pl.when(jnp.logical_and(tau >= 0, tau < total))
        def _():
            o_copy(tau).wait()

            @pl.when(tau + 1 < total)
            def _():
                o_copy(tau + 1).start()

            pbuf[tau % SLOTS_P] = dot(obuf[(tau // tiles) % 2], wout[tau % 2])

            @pl.when(is_end)
            def _():
                p_copy(tau).start()

        @pl.when(jnp.logical_and(is_mid, jnp.logical_and(tau >= LAG_PAIR, tau < total + LAG_PAIR)))
        def _():
            k = tau - LAG_PAIR
            p_copy(k).wait_recv()
            pbuf[k % SLOTS_P] = pbuf[k % SLOTS_P] + r1[k % SLOTS_1]
            a_copy(k).start()

        @pl.when(jnp.logical_and(is_mid, jnp.logical_and(tau >= LAG_MID, tau < total + LAG_MID)))
        def _():
            k = tau - LAG_MID
            a_copy(k).wait()

            @pl.when(k >= SLOTS_T)
            def _():
                t_copy(k - SLOTS_T).wait_send()

            value = pbuf[k % SLOTS_P] + r2[k % SLOTS_2]
            tbuf[k % SLOTS_T] = value
            t_copy(k).start()
            finish_tile(k, value)

        @pl.when(jnp.logical_and(is_end, jnp.logical_and(tau >= LAG_END, tau < total + LAG_END)))
        def _():
            k = tau - LAG_END
            t_copy(k).wait_recv()
            finish_tile(k, r3[k % SLOTS_3])

        @pl.when(seq < num_seqs)
        def _():
            @pl.when(t == 0)
            def _():
                x_copy(seq).start()
                for c in a_copies(0):
                    c.start()
                for c in b_copies(0):
                    c.start()
                x_copy(seq).wait()
                normalize()

            @pl.when(t < units // 2)
            def _():
                def two(j, carry):
                    a_step(2 * t + j)
                    return carry
                lax.fori_loop(0, 2, two, 0)

            @pl.when(t == units // 2 - 1)
            def _():
                finish_latents()

            @pl.when(t >= tiles - pairs)
            def _():
                b_step(t - (tiles - pairs), seq % 2)

    def stats_round(i):
        first = num_seqs * tiles
        for r in range(4):
            @pl.when(i == first + r)
            def _(r=r):
                if r > 0:
                    st_copy(r - 1).wait()
                    smax[...] = jnp.maximum(smax[...], srecv[r - 1])
                if r < 3:
                    st_copy(r).start()
                else:
                    gmine[...] = smax[...]
                    gall[z] = smax[...]
                    for d in range(3):
                        g_copy(d).start()

        @pl.when(i == first + 6)
        def _():
            for d in range(3):
                g_copy(d).wait()

    def whole_tick(i, carry):
        tick(i)
        stats_round(i)
        return carry

    lax.fori_loop(0, tiles + total + 7, whole_tick, 0)

    @pl.when(is_mid)
    def _():
        for k in range(total - SLOTS_T, total):
            t_copy(k).wait_send()
    for k in range(total - 2, total):
        yt_copy(k).wait()


def solution(mesh):
    def device_step(hidden, gain_in, gain_q, gain_kv, w_qa, w_kva, w_qb, w_kvb, w_out):
        num_seqs, seq_len, model_dim = hidden.shape
        q_rank, kv_rank = gain_q.shape[0], gain_kv.shape[0]
        rope_dim = w_kva.shape[1] - kv_rank
        num_heads = (w_qb.shape[1] - w_kvb.shape[1] + w_out.shape[0]) // rope_dim
        value_dim = w_out.shape[0] // num_heads
        nope_dim = w_kvb.shape[1] // num_heads - value_dim
        scale = (nope_dim + rope_dim) ** -0.5 * MSCALE_SQ
        cos, sin = rope_tables(seq_len, rope_dim)
        any_spec = pl.BlockSpec(memory_space=pl.ANY)
        vmem = pl.BlockSpec(memory_space=pltpu.VMEM)
        dma = pltpu.SemaphoreType.DMA
        block = (seq_len, TILE)
        y, gall, gmine = pl.pallas_call(
            lambda *refs: kernel((num_seqs, seq_len, model_dim, scale, rope_dim), *refs),
            out_shape=(jax.ShapeDtypeStruct(hidden.shape, BF16), jax.ShapeDtypeStruct((4, num_heads, 128), F32), jax.ShapeDtypeStruct((num_heads, 128), F32)),
            in_specs=[any_spec] + [vmem] * 5 + [any_spec] * 5,
            out_specs=(any_spec, vmem, vmem),
            scratch_shapes=[
                pltpu.VMEM((seq_len, model_dim), BF16),
                pltpu.VMEM((seq_len, q_rank), F32),
                pltpu.VMEM((seq_len, w_kva.shape[1]), F32),
                pltpu.VMEM((seq_len, q_rank), BF16),
                pltpu.VMEM((seq_len, kv_rank), BF16),
                pltpu.VMEM((seq_len, 128), BF16),
                pltpu.VMEM((2, seq_len, w_out.shape[0]), BF16),
                pltpu.VMEM((2, DEPTH, q_rank), BF16),
                pltpu.VMEM((2, DEPTH, w_kva.shape[1]), BF16),
                pltpu.VMEM((2, q_rank, 384), BF16),
                pltpu.VMEM((2, kv_rank, 512), BF16),
                pltpu.VMEM((2, w_out.shape[0], TILE), BF16),
                pltpu.VMEM((SLOTS_P,) + block, F32),
                pltpu.VMEM((SLOTS_1,) + block, F32),
                pltpu.VMEM((SLOTS_2,) + block, F32),
                pltpu.VMEM((SLOTS_3,) + block, F32),
                pltpu.VMEM((SLOTS_T,) + block, F32),
                pltpu.VMEM(block, BF16),
                pltpu.VMEM((2,) + block, BF16),
                pltpu.VMEM((num_heads, 128), F32),
                pltpu.VMEM((3, num_heads, 128), F32),
                dma, dma((2, 2)), dma((2, 2)), dma((2,)), dma, dma((2,)),
                dma((SLOTS_P,)), dma((SLOTS_1,)), dma((SLOTS_P,)), dma((SLOTS_2,)), dma((SLOTS_T,)), dma((SLOTS_3,)),
                dma((3,)), dma((3,)), dma((3,)), dma((3,)),
            ],
            compiler_params=pltpu.CompilerParams(collective_id=0, has_side_effects=True, vmem_limit_bytes=66 * 1000 * 1000),
            name="latent_attention",
        )(hidden, gain_in[None], gain_q[None], gain_kv[None], cos, sin, w_qa, w_kva, w_qb, w_kvb, w_out)
        head_max = gmine[:, 0]
        clip_gain = CLIP_TAU / jnp.maximum(CLIP_TAU, head_max)
        root_gain = jnp.sqrt(clip_gain)
        new_qb = rescale(w_qb, column_gains(root_gain, nope_dim, clip_gain, rope_dim))
        new_kvb = rescale(w_kvb, column_gains(root_gain, nope_dim, jnp.ones_like(clip_gain), value_dim))
        return y, gall[:, :, 0].reshape(-1), new_qb, new_kvb

    weight_spec = P(None, 'tp')
    return jax.shard_map(device_step, mesh=mesh, in_specs=(P('dp', None, None), P(), P(), P(), P(), P(), weight_spec, weight_spec, P('tp', None)), out_specs=(P('dp', None, None), P(), weight_spec, weight_spec), check_vma=False)
```

time: 2060 us -> 1080 us (0.52)
  waiting for transfers between devices: 1310 us -> 0 us
  Pallas kernels: 0 us -> 1020 us
  matrix products: 439 us -> 0 us
  other arithmetic: 203 us -> 31.4 us
  local copies, waits for them, and re-layouts: 52 us -> 19.3 us
  blocking collectives: 30.6 us -> 0 us
    psum x1 -> x0, waiting for transfers between devices: 1310 us -> none  [device_step(): head_sum = lax.psum(head_part, 'tp')]
    pallas_call x0 -> x1, Pallas kernels: none -> 1020 us  [device_step(): pl.pallas_call(lambda *refs: kernel((num_seqs, seq_len, model_dim, scale,...]
    dot_general x8 -> x0, matrix products: 439 us -> none  [the longest x1 103 us: device_step(): jnp.einsum('bqhd,bkhd->bhqk', q_nope, kv_full[..., :nope_dim], preferred_...]
    sub x1 -> x0, other arithmetic: 129 us -> none  [device_step(): attn_prob = jax.nn.softmax(logits, axis=-1).astype(jnp.bfloat16)]
    convert_element_type x4 -> x3, other arithmetic: 54.7 us -> 28.6 us  [the longest x2 28.6 us: rescale(): return (weight.astype(F32) * col_gain[None, :]).astype(BF16)]
    slice x1, local copies, waits for them, and re-layouts: 24.2 us -> 0.94 us  [device_step(): return (y, gall[:, :, 0].reshape(-1), new_qb, new_kvb)]
  transfers between devices with their start and end apart: 1 -> 0, of which waited for: 1 -> 0; matrix products, arithmetic and copies ran while one was open for 1% -> 0% of each run, Pallas kernels for 0% -> 0%
where the time goes in v1:
time: 1080 us
  Pallas kernels  1020 us (94%)
  other arithmetic  31.4 us (3%)
  local copies, waits for them, and re-layouts  19.3 us (2%)
    pallas_call x1, Pallas kernels, device_step(): pl.pallas_call(lambda *refs: kernel((num_seqs, seq_len, model_dim, scale,...  1020 us
    convert_element_type x2, other arithmetic, rescale(): return (weight.astype(F32) * col_gain[None, :]).astype(BF16)  28.6 us

profile of v1, /device:TPU:0, one launch (start us, length us, event | category | flops | bytes accessed | tf_op | source)
XLA Modules:
  0.0 1075.3 jit_solution(6388830571792185094)
XLA Ops:
  0.6 0.1 pad.8.clone
  0.7 1.3 broadcast_in_dim.17.refs_2_
  2.0 1.0 fusion
  3.0 1.0 maximum_maximum_fusion.1
  4.0 8.6 copy.16.refs_7_
  12.7 1023.9 %latent_attention.1 = (bf16[4,512,5120]{2,1,0:T(8,128)(2,1)}, f32[4,32,128]{2,1,0:T(8,128)}, f32[32,128]{1,0:T(8,128)}) custom-call(bf16[4,512,5120]{2,1,0:T(8,128)(2,1)} %refs_0_.1, f32[1,5120]{1,0:T(1,128)} %bitcast.6, f32[1,1536]{1,0:T(1,128)} %broadcast_in_dim.17.refs_2_, f32[1,512]{1,0:T(1,128)} %bitcast.7, f32[512,128]{1,0:T(8,128)} %get-tuple-element.16.refs_4_, ...), custom_call_target="tpu_custom_call" | custom-call | tf_op jit(solution)/shard_map/latent_attention/pallas_call | solution.py:364
  1036.5 0.8 sqrt_reduce_fusion
  1037.4 0.9 slice_reduce_fusion
  1038.3 0.6 reshape_squeeze.3
  1038.9 0.1 broadcast_in_dim.39
  1039.0 0.1 broadcast_in_dim.41
  1039.1 0.1 mul.57
  1039.2 8.9 multiply_convert_fusion.1
  1048.2 0.0 copy-start
  1048.2 19.6 %multiply_convert_fusion = bf16[1536,6144]{1,0:T(8,128)(2,1)} fusion(bf16[1536,6144]{1,0:T(8,128)(2,1)} %refs_8_.1, f32[6144]{0:T(1024)S(1)} %mul.57), kind=kLoop, calls=%fused_computation | loop fusion | flops 28311552 | bytes 37773312 | tf_op jit(solution)/shard_map/convert_element_type | solution.py:37
  1067.8 0.0 copy-done
  1067.8 7.5 copy.19
  (6 shorter events, 0.0 us)
Async XLA Ops:
  1048.2 19.6 %copy-start = (bf16[4,512,5120]{2,1,0:T(8,128)(2,1)S(1)}, bf16[4,512,5120]{2,1,0:T(8,128)(2,1)}, u32[]{:S(2)}) copy-start(bf16[4,512,5120]{2,1,0:T(8,128)(2,1)} %get-tuple-element.21) | copy-start | bytes 62914564

commit v2 on v1

--- a/solution.py
+++ b/solution.py
@@ -14,8 +14,10 @@
 F32 = jnp.float32
 BF16 = jnp.bfloat16
 
-TILE = 256
+ROWS = 256
+TILE = 512
 DEPTH = 512
+A_TICKS = 2
 LAG_PAIR, LAG_MID, LAG_END = 2, 4, 6
 SLOTS_P, SLOTS_1, SLOTS_2, SLOTS_3, SLOTS_T = 5, 7, 6, 7, 3
 
@@ -28,17 +30,29 @@
     return jnp.concatenate([cos, cos, blank], axis=1), jnp.concatenate([-sin, sin, blank], axis=1)
 
 
-def column_gains(first_gain, first_dim, second_gain, second_dim):
-    num_heads = first_gain.shape[0]
-    return jnp.concatenate([jnp.broadcast_to(first_gain[:, None], (num_heads, first_dim)), jnp.broadcast_to(second_gain[:, None], (num_heads, second_dim))], axis=1).reshape(-1)
-
-
-def rescale(weight, col_gain):
-    return (weight.astype(F32) * col_gain[None, :]).astype(BF16)
+def clip_kernel(top, qb, kvb, y, new_qb, new_kvb, new_y):
+    pair = pl.program_id(0)
+    g0 = CLIP_TAU / jnp.maximum(CLIP_TAU, top[pl.ds(pair * 2, 1), :])
+    g1 = CLIP_TAU / jnp.maximum(CLIP_TAU, top[pl.ds(pair * 2 + 1, 1), :])
+    s0, s1 = jnp.sqrt(g0), jnp.sqrt(g1)
+    low = lax.broadcasted_iota(jnp.int32, (1, 128), 1) < 64
+    for j, gain in enumerate((s0, jnp.where(low, g0, s1), jnp.where(low, s1, g1))):
+        cols = slice(j * 128, (j + 1) * 128)
+        new_qb[:, cols] = (qb[:, cols].astype(F32) * gain).astype(BF16)
+    for j, gain in ((0, s0), (2, s1)):
+        cols = slice(j * 128, (j + 1) * 128)
+        new_kvb[:, cols] = (kvb[:, cols].astype(F32) * gain).astype(BF16)
+        cols = slice((j + 1) * 128, (j + 2) * 128)
+        new_kvb[:, cols] = kvb[:, cols]
+    new_y[...] = y[...]
 
 
 def dot(a, b):
     return jnp.dot(a, b, preferred_element_type=F32)
+
+
+def dot_t(a, b):
+    return lax.dot_general(a, b, (((1,), (1,)), ((), ())), preferred_element_type=F32)
 
 
 def kernel(dims, x_hbm, gin, gq, gkv, cos, sin, wqa_hbm, wkva_hbm, wqb_hbm, wkvb_hbm, wout_hbm,
@@ -53,7 +67,9 @@
     tiles = model_dim // TILE
     units = model_dim // DEPTH
     pairs = wqb_hbm.shape[1] // 384
-    total = num_seqs * tiles
+    halves = seq_len // ROWS
+    chunks = num_seqs * halves
+    total = chunks * tiles
     z = lax.axis_index("tp")
     dp = lax.axis_index("dp")
     is_mid = jnp.logical_or(z == 1, z == 2)
@@ -70,14 +86,17 @@
         pl.semaphore_signal(barrier, inc=1, device_id={"tp": peer}, device_id_type=MESH)
     pl.semaphore_wait(barrier, 6)
 
-    def x_copy(seq):
-        return pltpu.make_async_copy(x_hbm.at[seq], xn, x_sem)
+    def rows_of(c):
+        return pl.ds(pl.multiple_of((c % halves) * ROWS, ROWS), ROWS)
+
+    def x_copy(c):
+        return pltpu.make_async_copy(x_hbm.at[c // halves, rows_of(c)], xn, x_sem)
 
     def a_copies(u):
         slot = u % 2
         rows = pl.ds(pl.multiple_of(u * DEPTH, DEPTH), DEPTH)
         return (pltpu.make_async_copy(wqa_hbm.at[rows], wqa.at[slot], a_sem.at[0, slot]),
-                pltpu.make_async_copy(wkva_hbm.at[rows], wkva.at[slot], a_sem.at[1, slot]))
+                pltpu.make_async_copy(wkva_hbm.at[:, rows], wkva.at[slot], a_sem.at[1, slot]))
 
     def b_copies(hp):
         slot = hp % 2
@@ -91,10 +110,10 @@
         return pltpu.make_async_copy(wout_hbm.at[:, cols_of(k)], wout.at[k % 2], o_sem.at[k % 2])
 
     def xt_copy(k):
-        return pltpu.make_async_copy(x_hbm.at[k // tiles, :, cols_of(k)], xt, xt_sem)
+        return pltpu.make_async_copy(x_hbm.at[k // (tiles * halves), rows_of(k // tiles), cols_of(k)], xt, xt_sem)
 
     def yt_copy(k):
-        return pltpu.make_async_copy(yt.at[k % 2], y_hbm.at[k // tiles, :, cols_of(k)], yt_sem.at[k % 2])
+        return pltpu.make_async_copy(yt.at[k % 2], y_hbm.at[k // (tiles * halves), rows_of(k // tiles), cols_of(k)], yt_sem.at[k % 2])
 
     def p_copy(k):
         return pltpu.make_async_remote_copy(
@@ -128,7 +147,7 @@
             inv = lax.rsqrt(jnp.mean(v * v, axis=-1, keepdims=True) + NORM_EPS)
             xn[rows, :] = (v * inv * gin[...]).astype(BF16)
             return carry
-        lax.fori_loop(0, seq_len // 16, block, 0)
+        lax.fori_loop(0, ROWS // 16, block, 0)
 
     def a_step(u):
         for c in a_copies(u):
@@ -148,13 +167,13 @@
         def _():
             for j in range(q_rank // width):
                 accq[:, j * width:(j + 1) * width] = dot(piece, wqa[slot, :, j * width:(j + 1) * width])
-            acck[...] = dot(piece, wkva[slot])
+            acck[...] = dot_t(piece, wkva[slot])
 
         @pl.when(u > 0)
         def _():
             for j in range(q_rank // width):
                 accq[:, j * width:(j + 1) * width] += dot(piece, wqa[slot, :, j * width:(j + 1) * width])
-            acck[...] += dot(piece, wkva[slot])
+            acck[...] += dot_t(piece, wkva[slot])
 
     def rope(v, c, s):
         half = rope_dim // 2
@@ -162,21 +181,22 @@
         swap = jnp.where(lane < half, pltpu.roll(v, 128 - half, 1), pltpu.roll(v, half, 1))
         return v * c + swap * s
 
-    def finish_latents():
+    def finish_latents(half):
         def block(i, carry):
             rows = pl.ds(pl.multiple_of(i * 64, 64), 64)
+            keys = pl.ds(pl.multiple_of(half * ROWS + i * 64, 64), 64)
             v = accq[rows, :]
             inv = lax.rsqrt(jnp.mean(v * v, axis=-1, keepdims=True) + NORM_EPS)
             cq[rows, :] = (v * inv * gq[...]).astype(BF16)
             w = acck[rows, :kv_rank]
             inv = lax.rsqrt(jnp.mean(w * w, axis=-1, keepdims=True) + NORM_EPS)
-            ckv[rows, :] = (w * inv * gkv[...]).astype(BF16)
+            ckv[keys, :] = (w * inv * gkv[...]).astype(BF16)
             kr = jnp.concatenate([acck[rows, kv_rank:], jnp.zeros((64, 128 - rope_dim), F32)], axis=1)
-            krot[rows, :] = rope(kr, cos[rows, :], sin[rows, :]).astype(BF16)
+            krot[keys, :] = rope(kr, cos[keys, :], sin[keys, :]).astype(BF16)
             return carry
-        lax.fori_loop(0, seq_len // 64, block, 0)
-
-    def b_step(hp, oslot):
+        lax.fori_loop(0, ROWS // 64, block, 0)
+
+    def b_step(hp, oslot, half):
         for c in b_copies(hp):
             c.wait()
 
@@ -186,31 +206,30 @@
                 c.start()
 
         slot = hp % 2
-        qf = dot(cq[...], wqb[slot])
-        kv = dot(ckv[...], wkvb[slot]).astype(BF16)
-        qs = pltpu.roll(qf, 192, 1)
-        blk = 256
-        for head, q2 in ((0, qf), (1, qs)):
-            q_rot = rope(q2[:, 128:256], cos[...], sin[...])
-            qcat = jnp.concatenate([q2[:, :128].astype(BF16), q_rot.astype(BF16)], axis=1)
-            kcat = jnp.concatenate([kv[:, head * 256:head * 256 + 128], krot[...]], axis=1)
-            vals = kv[:, head * 256 + 128:head * 256 + 256]
-            best = None
-            for i in range(seq_len // blk):
-                width = (i + 1) * blk
-                l = lax.dot_general(qcat[i * blk:width], kcat[:width], (((1,), (1,)), ((), ())), preferred_element_type=F32) * scale
-                row = lax.broadcasted_iota(jnp.int32, l.shape, 0) + i * blk
-                col = lax.broadcasted_iota(jnp.int32, l.shape, 1)
-                l = jnp.where(col <= row, l, -jnp.inf)
-                m = jnp.max(l, axis=-1, keepdims=True)
-                e = jnp.exp(l - m)
-                p = (e * (1.0 / jnp.sum(e, axis=-1, keepdims=True))).astype(BF16)
-                o = dot(p, vals[:width]).astype(BF16)
-                obuf[oslot, i * blk:width, pl.ds(pl.multiple_of(hp * 256 + head * 128, 128), 128)] = o
-                top = jnp.max(m, axis=0, keepdims=True)
-                best = top if best is None else jnp.maximum(best, top)
-            r = pl.ds(hp * 2 + head, 1)
-            smax[r, :] = jnp.maximum(smax[r, :], jnp.broadcast_to(best, (1, 128)))
+        for h in range(halves):
+            @pl.when(half == h)
+            def _(h=h):
+                width = (h + 1) * ROWS
+                mine = slice(h * ROWS, width)
+                qf = dot(cq[...], wqb[slot])
+                kv = dot(ckv[:width, :], wkvb[slot]).astype(BF16)
+                qs = pltpu.roll(qf, 192, 1)
+                for head, q2 in ((0, qf), (1, qs)):
+                    q_rot = rope(q2[:, 128:256], cos[mine, :], sin[mine, :])
+                    qcat = jnp.concatenate([q2[:, :128].astype(BF16), q_rot.astype(BF16)], axis=1)
+                    kcat = jnp.concatenate([kv[:, head * 256:head * 256 + 128], krot[:width, :]], axis=1)
+                    l = dot_t(qcat, kcat) * scale
+                    row = lax.broadcasted_iota(jnp.int32, l.shape, 0) + h * ROWS
+                    col = lax.broadcasted_iota(jnp.int32, l.shape, 1)
+                    l = jnp.where(col <= row, l, -jnp.inf)
+                    m = jnp.max(l, axis=-1, keepdims=True)
+                    e = jnp.exp(l - m)
+                    p = (e * (1.0 / jnp.sum(e, axis=-1, keepdims=True))).astype(BF16)
+                    o = dot(p, kv[:, head * 256 + 128:head * 256 + 256]).astype(BF16)
+                    obuf[oslot, :, pl.ds(pl.multiple_of(hp * 256 + head * 128, 128), 128)] = o
+                    best = jnp.max(m, axis=0, keepdims=True)
+                    r = pl.ds(hp * 2 + head, 1)
+                    smax[r, :] = jnp.maximum(smax[r, :], jnp.broadcast_to(best, (1, 128)))
 
     def finish_tile(k, value):
         xt_copy(k).wait()
@@ -225,7 +244,7 @@
     smax[...] = jnp.full(smax.shape, -jnp.inf, F32)
 
     def tick(i):
-        seq = i // tiles
+        chunk = i // tiles
         t = i % tiles
         tau = i - tiles
 
@@ -284,35 +303,40 @@
             t_copy(k).wait_recv()
             finish_tile(k, r3[k % SLOTS_3])
 
-        @pl.when(seq < num_seqs)
-        def _():
+        @pl.when(chunk < chunks)
+        def _():
+            half = chunk % halves
+
             @pl.when(t == 0)
             def _():
-                x_copy(seq).start()
+                x_copy(chunk).start()
                 for c in a_copies(0):
                     c.start()
                 for c in b_copies(0):
                     c.start()
-                x_copy(seq).wait()
+                x_copy(chunk).wait()
                 normalize()
 
-            @pl.when(t < units // 2)
-            def _():
-                def two(j, carry):
-                    a_step(2 * t + j)
+            @pl.when(t < A_TICKS)
+            def _():
+                def step(j, carry):
+                    a_step(t * (units // A_TICKS) + j)
                     return carry
-                lax.fori_loop(0, 2, two, 0)
-
-            @pl.when(t == units // 2 - 1)
-            def _():
-                finish_latents()
-
-            @pl.when(t >= tiles - pairs)
-            def _():
-                b_step(t - (tiles - pairs), seq % 2)
+                lax.fori_loop(0, units // A_TICKS, step, 0)
+
+            @pl.when(t == A_TICKS - 1)
+            def _():
+                finish_latents(half)
+
+            @pl.when(t >= A_TICKS)
+            def _():
+                def step(j, carry):
+                    b_step((t - A_TICKS) * (pairs // (tiles - A_TICKS)) + j, chunk % 2, half)
+                    return carry
+                lax.fori_loop(0, pairs // (tiles - A_TICKS), step, 0)
 
     def stats_round(i):
-        first = num_seqs * tiles
+        first = total
         for r in range(4):
             @pl.when(i == first + r)
             def _(r=r):
@@ -360,22 +384,22 @@
         any_spec = pl.BlockSpec(memory_space=pl.ANY)
         vmem = pl.BlockSpec(memory_space=pltpu.VMEM)
         dma = pltpu.SemaphoreType.DMA
-        block = (seq_len, TILE)
+        block = (ROWS, TILE)
         y, gall, gmine = pl.pallas_call(
             lambda *refs: kernel((num_seqs, seq_len, model_dim, scale, rope_dim), *refs),
             out_shape=(jax.ShapeDtypeStruct(hidden.shape, BF16), jax.ShapeDtypeStruct((4, num_heads, 128), F32), jax.ShapeDtypeStruct((num_heads, 128), F32)),
             in_specs=[any_spec] + [vmem] * 5 + [any_spec] * 5,
             out_specs=(any_spec, vmem, vmem),
             scratch_shapes=[
-                pltpu.VMEM((seq_len, model_dim), BF16),
-                pltpu.VMEM((seq_len, q_rank), F32),
-                pltpu.VMEM((seq_len, w_kva.shape[1]), F32),
-                pltpu.VMEM((seq_len, q_rank), BF16),
+                pltpu.VMEM((ROWS, model_dim), BF16),
+                pltpu.VMEM((ROWS, q_rank), F32),
+                pltpu.VMEM((ROWS, w_kva.shape[1]), F32),
+                pltpu.VMEM((ROWS, q_rank), BF16),
                 pltpu.VMEM((seq_len, kv_rank), BF16),
                 pltpu.VMEM((seq_len, 128), BF16),
-                pltpu.VMEM((2, seq_len, w_out.shape[0]), BF16),
+                pltpu.VMEM((2, ROWS, w_out.shape[0]), BF16),
                 pltpu.VMEM((2, DEPTH, q_rank), BF16),
-                pltpu.VMEM((2, DEPTH, w_kva.shape[1]), BF16),
+                pltpu.VMEM((2, w_kva.shape[1], DEPTH), BF16),
                 pltpu.VMEM((2, q_rank, 384), BF16),
                 pltpu.VMEM((2, kv_rank, 512), BF16),
                 pltpu.VMEM((2, w_out.shape[0], TILE), BF16),
@@ -394,13 +418,23 @@
             ],
             compiler_params=pltpu.CompilerParams(collective_id=0, has_side_effects=True, vmem_limit_bytes=66 * 1000 * 1000),
             name="latent_attention",
-        )(hidden, gain_in[None], gain_q[None], gain_kv[None], cos, sin, w_qa, w_kva, w_qb, w_kvb, w_out)
-        head_max = gmine[:, 0]
-        clip_gain = CLIP_TAU / jnp.maximum(CLIP_TAU, head_max)
-        root_gain = jnp.sqrt(clip_gain)
-        new_qb = rescale(w_qb, column_gains(root_gain, nope_dim, clip_gain, rope_dim))
-        new_kvb = rescale(w_kvb, column_gains(root_gain, nope_dim, jnp.ones_like(clip_gain), value_dim))
-        return y, gall[:, :, 0].reshape(-1), new_qb, new_kvb
+        )(hidden, gain_in[None], gain_q[None], gain_kv[None], cos, sin, w_qa, w_kva.T, w_qb, w_kvb, w_out)
+        pairs = num_heads // 2
+        y = y.reshape(num_seqs * seq_len, model_dim)
+        share = y.shape[0] // pairs
+        qb_block = pl.BlockSpec((q_rank, 384), lambda i: (0, i))
+        kvb_block = pl.BlockSpec((kv_rank, 512), lambda i: (0, i))
+        y_block = pl.BlockSpec((share, model_dim), lambda i: (i, 0))
+        new_qb, new_kvb, y = pl.pallas_call(
+            clip_kernel,
+            grid=(pairs,),
+            out_shape=(jax.ShapeDtypeStruct(w_qb.shape, BF16), jax.ShapeDtypeStruct(w_kvb.shape, BF16), jax.ShapeDtypeStruct(y.shape, BF16)),
+            in_specs=[pl.BlockSpec((num_heads, 128), lambda i: (0, 0)), qb_block, kvb_block, y_block],
+            out_specs=(qb_block, kvb_block, y_block),
+            compiler_params=pltpu.CompilerParams(vmem_limit_bytes=32 * 1024 * 1024),
+            name="clip_weights",
+        )(gmine, w_qb, w_kvb, y)
+        return y.reshape(hidden.shape), gall[:, :, 0].reshape(-1), new_qb, new_kvb
 
     weight_spec = P(None, 'tp')
     return jax.shard_map(device_step, mesh=mesh, in_specs=(P('dp', None, None), P(), P(), P(), P(), P(), weight_spec, weight_spec, P('tp', None)), out_specs=(P('dp', None, None), P(), weight_spec, weight_spec), check_vma=False)

time: 1080 us -> 1040 us (0.963)
  other arithmetic: 31.4 us -> 2 us
  local copies, waits for them, and re-layouts: 19.3 us -> 7.01 us
    pallas_call x0 -> x1, Pallas kernels: none -> 33.5 us  [device_step(): pl.pallas_call(clip_kernel, grid=(pairs,), out_shape=(jax.ShapeDtypeStruc...]
    pallas_call x1, Pallas kernels: 1020 us -> 995 us  [device_step(): pl.pallas_call(lambda *refs: kernel((num_seqs, seq_len, model_dim, scale,...]
    convert_element_type x2 -> x0, other arithmetic: 28.6 us -> none  [rescale(): return (weight.astype(F32) * col_gain[None, :]).astype(BF16)]
    unnamed x6 -> x4, local copies, waits for them, and re-layouts: 16.2 us -> 4.1 us
where the time goes in v2:
time: 1040 us
  Pallas kernels  1030 us (99%)
    pallas_call x1, Pallas kernels, device_step(): pl.pallas_call(lambda *refs: kernel((num_seqs, seq_len, model_dim, scale,...  995 us
    pallas_call x1, Pallas kernels, device_step(): pl.pallas_call(clip_kernel, grid=(pairs,), out_shape=(jax.ShapeDtypeStruc...  33.5 us

profile of v2, /device:TPU:0, one launch (start us, length us, event | category | flops | bytes accessed | tf_op | source)
XLA Modules:
  0.0 1038.4 jit_solution(2589974553549670028)
XLA Ops:
  0.6 0.1 pad.5.clone
  0.7 1.3 broadcast_in_dim.15.refs_2_
  2.0 1.0 fusion
  3.0 1.0 maximum_maximum_fusion.1
  4.0 995.2 %latent_attention.1 = (bf16[4,512,5120]{2,1,0:T(8,128)(2,1)}, f32[4,32,128]{2,1,0:T(8,128)}, f32[32,128]{1,0:T(8,128)}) custom-call(bf16[4,512,5120]{2,1,0:T(8,128)(2,1)} %refs_0_.1, f32[1,5120]{1,0:T(1,128)} %bitcast.7, f32[1,1536]{1,0:T(1,128)} %broadcast_in_dim.15.refs_2_, f32[1,512]{1,0:T(1,128)} %bitcast.8, f32[512,128]{1,0:T(8,128)} %get-tuple-element.20.refs_4_, ...), custom_call_target="tpu_custom_call" | custom-call | tf_op jit(solution)/shard_map/latent_attention/pallas_call | solution.py:388
  999.3 0.9 slice_reduce_fusion
  1000.2 0.6 reshape_squeeze.3
  1000.8 0.0 copy-start
  1000.8 3.4 copy-done
  1004.2 0.0 copy-start.1
  1004.2 0.7 copy-done.1
  1004.9 33.5 %clip_weights.1 = (bf16[1536,6144]{1,0:T(8,128)(2,1)}, bf16[512,8192]{1,0:T(8,128)(2,1)}, bf16[2048,5120]{1,0:T(8,128)(2,1)}) custom-call(f32[32,128]{1,0:T(8,128)S(1)} %copy-done.1, bf16[1536,6144]{1,0:T(8,128)(2,1)} %qb.1, bf16[512,8192]{1,0:T(8,128)(2,1)S(1)} %copy-done, bf16[2048,5120]{1,0:T(8,128)(2,1)} %bitcast.5), custom_call_target="tpu_custom_call" | custom-call | tf_op jit(solution)/shard_map/clip_weights/pallas_call | solution.py:428
  (3 shorter events, 0.0 us)
Async XLA Ops:
  1000.8 3.4 copy-start
  1004.2 0.7 copy-start.1
